TPU v7x, 256 devices: a whole 4x4x8 slice. The times are simulated.
256 devices in a mesh: seq: 32 (over z, y), head: 8 (over x, core).
Axes of the slice: x: 4, y: 4, z: 8, core: 2. Of those that a mesh axis runs over, the one named last changes fastest.
Arguments:
- queries: bfloat16 [32768, 12288], P(('seq', 'head')), may hold values from -8 to 8
- latent: bfloat16 [32768, 512], P(('seq', 'head')), may hold values from -6 to 6
- rope_keys: bfloat16 [32768, 64], P(('seq', 'head')), may hold values from -8 to 8
- key_weight: bfloat16 [512, 8192], P('seq', 'head'), may hold values from -0.25 to 0.25
- value_weight: bfloat16 [512, 8192], P('seq', 'head'), may hold values from -0.25 to 0.25
- doc_lengths: int32 [128], replicated, may hold values from 1 to 510, as said below
Outputs:
- attended: bfloat16 [32768, 8192], P(('seq', 'head'))
Inputs may be any that keep to these rules, and one draw needn't show every extreme that they name: `doc_lengths`: the documents lie in order in the pack and their lengths sum to 32768; document 0 starts at position 0 and every other document d starts strictly inside positions d * 256 to (d + 1) * 256 - 1, excluding the first of these; one length is exactly 510.
All inputs are finite; a program needn't handle non-finite values.
Results may differ from a plain program's by a relative error of at most 0.0062.
Values may be sent and summed in bfloat16 or wider, within the bound.
A program may use at most 64 MiB of HBM per device.

v0:
```python
import collections
import functools
import math

import jax
import jax.numpy as jnp
from jax import lax
from jax.experimental import pallas as pl
from jax.experimental.pallas import tpu as pltpu
from jax.sharding import PartitionSpec as P

NOPE = 128
ROPE = 64
VDIM = 128
QK = NOPE + ROPE
LOG2E = 1.4426950408889634
NY = 4

MESH = pl.DeviceIdType.MESH

Stage = collections.namedtuple(
    "Stage", ("last", "far", "near_way", "far_way", "upwards", "split_side", "split_z")
)
STAGES = (
    Stage('x', 4, 0, -1, 1, 0, 0),
    Stage('y', 0, 0, 0, 4, 0, 1),
    Stage('y', 4, 0, -1, 6, 0, 1),
    Stage('x', 0, 0, 1, 4, 0, 0),
)
RANKS = (
    dict(near=11, z=4, far=7, farz=17, over=23, side=2),
    dict(near=6, z=0, far=9, farz=1, over=13, side=18),
    dict(near=12, z=21, far=19, farz=3, over=10, side=20),
    dict(near=16, z=14, far=24, farz=8, over=22, side=5),
)
LATENT_RANK = 15
UNITS = 4
RATE = 46.6e3
LATENCY = 3.0
HOP = 0.8
D2D_RATE = 300e3
BACKLOG = 1.0
SEND_COST = 0.04
WAIT_COST = 0.02
BLOCK = 0.8
DRAIN = (0.6, 0.5, 0.35)
DEPTH = 3
OFFSETS = (0, -1, 1, 2)
CHUNK = 32


class Message:
    def __init__(self, name, group, kind, deps, link, size, priority, units=None, where=None, move=None, hops=1):
        self.name, self.group, self.kind, self.deps, self.link = name, group, kind, deps, link
        self.size, self.priority, self.units, self.where = size, priority, units, where
        self.move, self.hops = move, hops


def weight_messages(nx, nz):
    tile = 16 * 128 * 2
    half = nz // 2
    found = []

    def add(name, group, kind, deps, axis, step, units, where, blocks):
        move = {"x": 0, "z": 0, "y": 0}
        move[axis] = step
        link = axis + ("+" if step > 0 else "-")
        rank = RANKS[name[0]][name[1]]
        found.append(Message(
            name, group, kind, deps, link, blocks * units[1] * tile, rank, units, where, move, abs(step)
        ))

    for s, stage in enumerate(STAGES):
        last, minor = stage.last, "y" if stage.last == "x" else "x"
        every, far = (UNITS * s, UNITS), (UNITS * s, stage.far)
        over = (UNITS * s + stage.far, UNITS - stage.far)

        def at(minor_at, last_at, z_at):
            return {minor: minor_at, last: last_at, "z": z_at}

        near = {k: (s, "near", k) for k in (1, -1, 2)}
        one_by_one = stage.near_way or stage.split_side or stage.split_z
        for k, name in near.items():
            group = name if one_by_one else (s, "near")
            if k == 2 and stage.near_way:
                way = stage.near_way
                add(name, group, "near", [near[way]], minor, way, every, at(-way, 0, 0), 1)
            else:
                add(name, group, "near", [], minor, k, every, at(0, 0, 0), 1)
        near = list(near.values())

        def first(name, group, kind, split, axis, way):
            if not split:
                add(name, group, kind, near, axis, way, every, at(None, 0, 0), 4)
                return [name]
            for k in (0, 1, -1, 2):
                add((*name, k), group, kind, [(s, "near", k)] if k else [], axis, way, every, at(-k, 0, 0), 1)
            return [(*name, k) for k in (0, 1, -1, 2)]

        reach = {1: half - s % 2, -1: half - 1 + s % 2}
        came = {0: near}
        for way in (1, -1):
            for d in range(1, reach[way] + 1):
                name = (s, "z", way, d)
                if d == 1:
                    came[-way] = first(name, name, "z", stage.split_z, "z", way)
                else:
                    add(name, name, "z", came[way * (1 - d)], "z", way, every, at(None, 0, way * (1 - d)), 4)
                    came[-way * d] = [name]
        if stage.far:
            name, way = (s, "far"), stage.far_way
            if way:
                deps = [(s, "side", way, 0, k) for k in (0, 1, -1, 2)] if stage.split_side else [(s, "side", way, 0)]
                add(name, name, "far", deps, last, way, far, at(None, -way, 0), 4)
            else:
                add(name, name, "far", near, last, 2, far, at(None, 0, 0), 4)
            for way in (1, -1):
                for d in range(1, reach[way] + 1):
                    deps = [(s, "far")] if d == 1 else [(s, "farz", way, d - 1)]
                    name = (s, "farz", way, d)
                    add(name, name, "far", deps, "z", way, far, at(None, 2, way * (1 - d)), 4)
        opposite = -half if s % 2 == 0 else half
        for i, r in enumerate((*range(0, -half, -1), opposite, *range(half - 1, 0, -1))):
            via = 1 if i < stage.upwards else -1
            for way in (1, -1):
                name = (s, "side", way, r)
                relayed = way == via and stage.far < UNITS
                alone = relayed or (r == 0 and stage.far and stage.far_way == way)
                group = name if alone else (s, "side", way, "rest")
                if r == 0:
                    names = first(name, group, "side", stage.split_side, last, way)
                else:
                    add(name, group, "side", came[r], last, way, every, at(None, 0, r), 4)
                    names = [name]
                if relayed:
                    deps = names
            if stage.far < UNITS:
                add((s, "over", via, r), (s, "over", via), "over", deps, last, via, over, at(None, -via, r), 4)
    return found


def latent_messages(tok, rank):
    size = tok * (rank + ROPE) * 2
    return [
        Message(("next",), ("next",), "latent", [], "x+", 1.3 * size, LATENT_RANK, hops=2),
        Message(("mate",), ("mate",), "latent", [], "d2d", size, LATENT_RANK),
        Message(("share",), ("share",), "latent", [("next",)], "d2d", size, LATENT_RANK),
    ]


def step_needs(messages, s, off):
    groups = {m.group for m in messages if m.name[0] == s}
    if STAGES[s].last == "y":
        return groups
    if off == 0:
        return {g for g in groups if g[1] in ("near", "z")}
    if off in (-1, 1):
        return {g for g in groups if g[1] == "side" and g[2] == -off}
    return {g for g in groups if g[1] in ("over", "far", "farz")}


def make_plan(messages):
    needs = {(s, off): step_needs(messages, s, off) for s in range(len(STAGES)) for off in OFFSETS}
    steps, able_steps, drained, prepared = [], [], 0, False
    group_of = {m.name: m.group for m in messages}
    left = {}
    for m in messages:
        left[m.group] = left.get(m.group, 0) + 1
    order, free, flying, seen = [], {}, [], set()
    waiting = sorted(messages, key=lambda m: m.priority)
    now = 0.0
    while waiting or flying or drained < DEPTH:
        flying.sort(key=lambda f: f[:2])
        if flying and flying[0][0] <= now:
            group = flying.pop(0)[2]
            left[group] -= 1
            if left[group] == 0:
                seen.add(group)
                order.append(("wait", group))
                now += WAIT_COST
                for step in [step for step, needed in needs.items() if needed <= seen]:
                    able_steps.append(step)
                    del needs[step]
            continue
        ready = [m for m in waiting if all(group_of[d] in seen for d in m.deps)]
        able = [m for m in ready if free.get(m.link, 0.0) - now < BACKLOG]
        if able:
            m = able[0]
            waiting.remove(m)
            order.append(("send", m.name))
            now += SEND_COST
            rate = D2D_RATE if m.link == "d2d" else RATE
            begun = max(now, free.get(m.link, 0.0))
            free[m.link] = begun + m.size * max(1, m.hops) / rate
            flying.append((free[m.link] + LATENCY + HOP * (m.hops - 1), len(order), m.group))
            continue
        if not prepared:
            if {("next",), ("mate",), ("share",)} <= seen:
                order.append(("piece", "setup"))
                now += BLOCK
                prepared = True
                continue
        elif able_steps:
            order.append(("piece", ("block", len(steps))))
            steps.append(able_steps.pop(0))
            now += BLOCK
            continue
        elif not needs and drained < DEPTH:
            order.append(("piece", ("block", len(steps) + drained)))
            now += DRAIN[drained]
            drained += 1
            continue
        times = [f[0] for f in flying[:1]] + [free[m.link] - BACKLOG for m in ready]
        now = max(now, min(times)) + 1e-6
    return order, steps, now


SEND_KINDS = ("near", "z", "far", "side", "over")


def kernel(
    sizes, queries, latent, rope, key_weight, value_weight, lengths, out,
    w, lat, rope_all, qbuf, kaug0, kaug1, rope_odd, vbuf0, vbuf1, sbuf0, sbuf1, pbuf0, pbuf1,
    inv0, inv1, bias, obuf, len_buf,
    own_sem, lat_sem, rope_sem, len_sem, lat_send, w_recv, w_send, q_sem, q_send, o_sem,
):
    n_seq, n_head, stages = sizes
    nx, ny, nz = n_head // 2, NY, n_seq // NY
    tok, rank = latent.shape
    keys = 4 * tok
    seq, head = lax.axis_index("seq"), lax.axis_index("head")
    x, core = head // 2, head % 2
    z, y = seq // ny, seq % ny
    mate = 2 * x + 1 - core
    slot = seq * nx + x
    after, before = (slot + 1) % (n_seq * nx), (slot + n_seq * nx - 1) % (n_seq * nx)

    messages = weight_messages(nx, nz)
    every = messages + latent_messages(tok, rank)
    order, turns, _ = make_plan(every)
    by_name = {m.name: m for m in every}
    groups = list(dict.fromkeys(m.group for m in messages))
    number = {g: i for i, g in enumerate(groups)}
    members = {g: [m for m in messages if m.group == g] for g in groups}
    sent_tiles = {kind: sum(m.size for m in messages if m.kind == kind) // 4096 for kind in SEND_KINDS}

    def device(dx, dy, dz):
        return ((z + dz) % nz) * ny + (y + dy) % ny, ((x + dx) % nx) * 2 + core

    def chip(which):
        return which // nx, (which % nx) * 2 + core

    barrier = pltpu.get_barrier_semaphore()
    peers = [device(k, 0, 0) for k in range(1, nx)] + [device(0, k, 0) for k in range(1, ny)]
    peers += [device(0, 0, 1), device(0, 0, nz - 1), (seq, mate), chip(after), chip(before)]
    for peer in peers:
        pl.semaphore_signal(barrier, inc=1, device_id=peer, device_id_type=MESH)

    for s in range(stages):
        for kv, source in enumerate((key_weight, value_weight)):
            for j in range(2):
                pltpu.make_async_copy(
                    source.at[:, pl.ds((2 * s + j) * 128, 128)],
                    w.at[UNITS * s + 2 * kv + j, x, z, y], own_sem.at[0],
                ).start()
    pltpu.make_async_copy(latent, lat.at[2 + core], lat_sem.at[2 + core]).start()
    pltpu.make_async_copy(rope, rope_all.at[2 + core], rope_sem.at[2 + core]).start()
    length_copy = pltpu.make_async_copy(lengths, len_buf, len_sem.at[0])
    length_copy.start()
    qw, cw = 2 * stages * QK, 2 * stages * VDIM

    def q_part(to_core, xi):
        return queries.at[:, pl.ds(pl.multiple_of((2 * xi + to_core) * qw, 128), qw)]

    for xi in range(nx):
        pltpu.make_async_copy(q_part(core, xi), qbuf.at[core, xi], q_sem.at[core]).start()

    def tiles(count):
        a, b, c, d = w.shape[:4]
        for k in range(1, d + 1):
            for j in range(1, c + 1):
                for i in range(1, b + 1):
                    if count % (i * j * k) == 0 and count // (i * j * k) <= a:
                        return w.at[pl.ds(0, count // (i * j * k)), pl.ds(0, i), pl.ds(0, j), pl.ds(0, k)]
        raise ValueError(count)

    def await_bytes(ref, sem):
        pltpu.make_async_copy(ref, ref, sem).wait()

    await_bytes(w.at[:, x, z, y], own_sem.at[0])
    pl.semaphore_wait(barrier, len(peers))

    def place(at, here, n):
        return pl.ds(0, n) if at is None else (here + at % n) % n

    def block(m, sent):
        def shifted(a):
            at = m.where[a]
            return at if at is None or sent else at - m.move[a]

        return w.at[
            pl.ds(*m.units), place(shifted("x"), x, nx), place(shifted("z"), z, nz), place(shifted("y"), y, ny)
        ]

    def remote(src, dst, send_sem, recv_sem, to):
        return pltpu.make_async_remote_copy(
            src_ref=src, dst_ref=dst, send_sem=send_sem, recv_sem=recv_sem,
            device_id=to, device_id_type=MESH,
        )

    def latent_copies(name):
        at = 2 + core if name == ("mate",) else core
        to = chip(after) if name == ("next",) else (seq, mate)
        shared = name == ("share",)
        return [
            remote(
                held.at[at] if shared else mine, held.at[at], lat_send.at[0], sems.at[at], to
            )
            for mine, held, sems in ((latent, lat, lat_sem), (rope, rope_all, rope_sem))
        ]

    def send(name):
        m = by_name[name]
        if m.kind == "latent":
            for copy in latent_copies(name):
                copy.start()
            return
        sent = block(m, True)
        remote(
            sent, sent, w_send.at[SEND_KINDS.index(m.kind)], w_recv.at[number[m.group]],
            device(m.move["x"], m.move["y"], m.move["z"]),
        ).start()

    def lat_wait(at):
        await_bytes(lat.at[at], lat_sem.at[at])
        await_bytes(rope_all.at[at], rope_sem.at[at])

    def take(group):
        if group == ("next",):
            lat_wait(core)
        elif group == ("mate",):
            lat_wait(3 - core)
        elif group == ("share",):
            lat_wait(1 - core)
        elif len(members[group]) == 1:
            await_bytes(block(members[group][0], False), w_recv.at[number[group]])
        else:
            count = sum(m.size for m in members[group]) // 4096
            await_bytes(tiles(count), w_recv.at[number[group]])

    def q_copy(xi):
        return remote(
            q_part(1 - core, xi), qbuf.at[core, xi], q_send.at[0], q_sem.at[core], (seq, mate)
        )

    def setup():
        lat_wait(2 + core)
        length_copy.wait()
        lane = lax.broadcasted_iota(jnp.int32, (1, lengths.shape[1]), 1)
        start_own = jnp.sum(jnp.where(lane < slot, len_buf[...], 0), axis=1, keepdims=True)
        start_last = jnp.sum(jnp.where(lane < slot - 1, len_buf[...], 0), axis=1, keepdims=True)
        first = slot * 2 * tok
        q_place = first + lax.broadcasted_iota(jnp.int32, (2 * tok, 1), 0)
        begun = jnp.where(q_place >= start_own, start_own, start_last)
        k_place = first - 2 * tok + lax.broadcasted_iota(jnp.int32, (2 * tok, keys), 1)
        bias[...] = jnp.where((k_place >= begun) & (k_place <= q_place), 0.0, -jnp.inf)
        for at in range(4):
            turned = rope_all[at].astype(jnp.float32)
            tail = jnp.concatenate([turned, jnp.zeros_like(turned)], axis=0).T
            rows = slice(at * tok, (at + 1) * tok)
            for kaug in (kaug0, kaug1):
                kaug[0, rows, NOPE:] = tail.astype(jnp.bfloat16)
            rope_odd[rows, :] = pltpu.roll(tail, ROPE, axis=1)
        for pbuf in (pbuf0, pbuf1):
            pbuf[:, :tok, 3 * tok:] = jnp.zeros((2, tok, tok), jnp.bfloat16)
        for t in range(2):
            await_bytes(qbuf.at[t], q_sem.at[t])

    scale = LOG2E / math.sqrt(QK)
    held = ((kaug0, vbuf0, sbuf0, pbuf0, inv0), (kaug1, vbuf1, sbuf1, pbuf1, inv1))

    codes = [s * nx + off % nx for s, off in turns]

    def where(k):
        if isinstance(k, int):
            code = codes[k]
        else:
            code = jnp.int32(codes[0])
            for i in range(1, len(codes)):
                code = jnp.where(k == i, codes[i], code)
        return code // nx, (x + code % nx) % nx

    def weights(s, j, xi):
        parts = [w[UNITS * s + j + i, xi].reshape(n_seq * 16, 128) for i in range(2)]
        return jnp.concatenate(parts, axis=1)

    def project_keys(k, parity):
        s, xi = where(k)
        kaug = held[parity][0]
        low = lax.broadcasted_iota(jnp.int32, (keys, NOPE), 1) < ROPE
        k = jnp.dot(lat[...].reshape(keys, rank), weights(s, 0, xi), preferred_element_type=jnp.float32)
        kaug[0, :, :NOPE] = k[:, :NOPE].astype(jnp.bfloat16)
        turned = pltpu.roll(k[:, NOPE:], ROPE, axis=1)
        kaug[1, :, :NOPE] = jnp.where(low, 0.0, turned).astype(jnp.bfloat16)
        kaug[1, :, NOPE:] = jnp.where(low, turned, rope_odd[...]).astype(jnp.bfloat16)

    def project_values(k, parity):
        s, xi = where(k)
        v = jnp.dot(lat[...].reshape(keys, rank), weights(s, 2, xi), preferred_element_type=jnp.float32)
        held[parity][1][...] = v.astype(jnp.bfloat16)

    def score(k, parity):
        s, xi = where(k)
        kaug, _, sbuf, _, _ = held[parity]
        for h in range(2):
            begin = pl.multiple_of(s * 2 * QK + h * NOPE, 128)
            q = qbuf[:, xi, :, pl.ds(begin, 2 * NOPE)].reshape(2 * tok, 2 * NOPE)
            sc = lax.dot_general(
                q, kaug[h], (((1,), (1,)), ((), ())), preferred_element_type=jnp.float32
            )
            for t in range(2):
                rows, span = slice(t * tok, (t + 1) * tok), (3 + t) * tok
                sbuf[h, rows, :span] = sc[rows, :span] * scale + bias[rows, :span]

    def soften(parity):
        _, _, sbuf, pbuf, inv = held[parity]
        for t in range(2):
            span = (3 + t) * tok
            for h in range(2):
                for r in range(0, tok, CHUNK):
                    rows = slice(t * tok + r, t * tok + r + CHUNK)
                    sc = sbuf[h, rows, :span]
                    expo = jnp.exp2(sc - jnp.max(sc, axis=1, keepdims=True))
                    total = jnp.sum(expo, axis=1, keepdims=True)
                    inv[h, rows, :] = jnp.broadcast_to(1.0 / total, (CHUNK, VDIM))
                    pbuf[h, rows, :span] = expo.astype(jnp.bfloat16)

    def mix(k, parity):
        s, xi = where(k)
        _, vbuf, _, pbuf, inv = held[parity]
        for h in range(2):
            cols = slice(h * VDIM, (h + 1) * VDIM)
            mixed = jnp.dot(pbuf[h], vbuf[:, cols], preferred_element_type=jnp.float32)
            mixed = (mixed * inv[h]).astype(jnp.bfloat16)
            low, high = mixed[:tok], mixed[tok:]
            at = pl.multiple_of((2 * xi + core) * cw + s * 2 * VDIM + h * VDIM, 128)
            out[:, pl.ds(at, VDIM)] = jnp.where(core == 0, low, high)
            obuf[s, xi, :, cols] = jnp.where(core == 0, high, low)

    def give(k):
        s, xi = where(k)
        at = pl.multiple_of((2 * xi + core) * cw + s * 2 * VDIM, 128)
        landed = out.at[:, pl.ds(at, 2 * VDIM)]
        remote(obuf.at[s, xi], landed, o_sem.at[0], o_sem.at[1], (seq, mate)).start()

    def act(kind, name):
        if kind == "send":
            send(name)
        else:
            take(name)

    steps = stages * nx
    between, current = {}, "setup"
    for kind, name in [("piece", "setup")] + order:
        if kind != "piece":
            between[current].append((kind, name))
        elif name == "setup":
            current = "setup" if not between else "ready"
            between[current] = []
        else:
            current = name
            between[current] = []

    def events(name):
        for kind, what in between[name]:
            act(kind, what)

    def events_of(j, low, high, back):
        if not any(between["block", DEPTH + 2 * k + back] for k in range(low, high)):
            return
        if high - low == 1:
            events(("block", DEPTH + 2 * low + back))
            return
        middle = (low + high) // 2
        pl.when(j < middle)(functools.partial(events_of, j, low, middle, back))
        pl.when(j >= middle)(functools.partial(events_of, j, middle, high, back))

    def run(b, turn, first, last):
        if first <= 1 <= last:
            score(b - 1, (turn - 1) % 2)
        if first <= 2 <= last:
            soften(turn % 2)
        if first <= 0 <= last:
            project_keys(b, turn % 2)
        if first <= 2 <= last:
            project_values(b - 2, turn % 2)
        if first <= 3 <= last:
            mix(b - 3, (turn - 3) % 2)
            give(b - 3)

    events("setup")
    for xi in range(nx):
        q_copy(xi).start()
    setup()
    events("ready")
    for b in range(DEPTH):
        run(b, b, 0, b)
        events(("block", b))
    pairs = (steps - DEPTH) // 2

    def pair(j, carry):
        for back in range(2):
            run(DEPTH + 2 * j + back, DEPTH + back, 0, DEPTH)
            events_of(j, 0, pairs, back)
        return carry

    lax.fori_loop(0, pairs, pair, 0)
    for b in range(DEPTH + 2 * pairs, steps + DEPTH):
        run(b, b, max(0, b - steps + 1), DEPTH)
        events(("block", b))

    for i, kind in enumerate(SEND_KINDS):
        await_bytes(tiles(sent_tiles[kind]), w_send.at[i])
    await_bytes(tiles(3 * tok * (rank + ROPE) * 2 // 4096), lat_send.at[0])
    await_bytes(qbuf.at[core], q_send.at[0])
    for i in range(2):
        await_bytes(obuf, o_sem.at[i])


def shards(queries, latent, rope_keys, key_weight, value_weight, doc_lengths):
    n_seq, n_head = lax.axis_size("seq"), lax.axis_size("head")
    nx = n_head // 2
    tok, rank = latent.shape
    stages = key_weight.shape[1] // (2 * NOPE)
    docs = doc_lengths.shape[0]
    count = len({m.group for m in weight_messages(nx, n_seq // NY)})
    dma = pltpu.SemaphoreType.DMA
    bf16 = jnp.bfloat16
    return pl.pallas_call(
        functools.partial(kernel, (n_seq, n_head, stages)),
        out_shape=jax.ShapeDtypeStruct((tok, n_head * stages * 2 * VDIM), bf16),
        in_specs=[pl.BlockSpec(memory_space=pltpu.HBM)] * 6,
        out_specs=pl.BlockSpec(memory_space=pltpu.VMEM),
        scratch_shapes=[
            pltpu.VMEM((UNITS * stages, nx, n_seq // NY, NY, key_weight.shape[0], 128), bf16),
            pltpu.VMEM((4, tok, rank), bf16),
            pltpu.VMEM((4, ROPE, tok), bf16),
            pltpu.VMEM((2, nx, tok, 2 * stages * QK), bf16),
            pltpu.VMEM((2, 4 * tok, 2 * NOPE), bf16),
            pltpu.VMEM((2, 4 * tok, 2 * NOPE), bf16),
            pltpu.VMEM((4 * tok, 2 * ROPE), jnp.float32),
            pltpu.VMEM((4 * tok, 2 * VDIM), bf16),
            pltpu.VMEM((4 * tok, 2 * VDIM), bf16),
            pltpu.VMEM((2, 2 * tok, 4 * tok), jnp.float32),
            pltpu.VMEM((2, 2 * tok, 4 * tok), jnp.float32),
            pltpu.VMEM((2, 2 * tok, 4 * tok), bf16),
            pltpu.VMEM((2, 2 * tok, 4 * tok), bf16),
            pltpu.VMEM((2, 2 * tok, VDIM), jnp.float32),
            pltpu.VMEM((2, 2 * tok, VDIM), jnp.float32),
            pltpu.VMEM((2 * tok, 4 * tok), jnp.float32),
            pltpu.VMEM((stages, nx, tok, 2 * VDIM), bf16),
            pltpu.VMEM((1, docs), jnp.int32),
            dma((1,)),
            dma((4,)),
            dma((4,)),
            dma((1,)),
            dma((1,)),
            dma((count,)),
            dma((len(SEND_KINDS),)),
            dma((2,)),
            dma((1,)),
            dma((2,)),
        ],
        compiler_params=pltpu.CompilerParams(
            collective_id=0, has_side_effects=True, vmem_limit_bytes=48 * 2**20
        ),
    )(*[
        pltpu.with_memory_space_constraint(a, pltpu.HBM)
        for a in (queries, latent, rope_keys.T, key_weight, value_weight, doc_lengths.reshape(1, docs))
    ])


def solution(mesh):
    placed = (
        P(("seq", "head"), None),
        P(("seq", "head"), None),
        P(("seq", "head"), None),
        P("seq", "head"),
        P("seq", "head"),
        P(),
    )
    return jax.shard_map(
        shards, mesh=mesh, in_specs=placed, out_specs=P(("seq", "head"), None), check_vma=False
    )
```

profile of v0, /device:TPU:1, one launch (start us, length us, event | category | flops | bytes accessed | tf_op | source)
XLA Modules:
  0.0 59.3 jit_solution(16589295512712534800)
XLA Ops:
  0.0 58.0 %shard_map.64 = bf16[128,8192]{1,0:T(8,128)(2,1)S(1)} custom-call(bf16[128,12288]{1,0:T(8,128)(2,1)} %queries.1, bf16[128,512]{1,0:T(8,128)(2,1)} %latent.1, bf16[64,128]{1,0:T(8,128)(2,1)} %bitcast.2, bf16[16,1024]{1,0:T(8,128)(2,1)} %key_weight.1, bf16[16,1024]{1,0:T(8,128)(2,1)} %value_weight.1, s32[1,128]{1,0:T(1,128)} %bitcast.3), custom_call_target="tpu_custom_call" | custom-call | tf_op jit(solution)/shard_map/pallas_call | solution.py:539
  58.0 1.3 %copy.8 = bf16[128,8192]{1,0:T(8,128)(2,1)} copy(bf16[128,8192]{1,0:T(8,128)(2,1)S(1)} %shard_map.64) | data formatting | bytes 4194304
where the time goes:
time: 59.4 us; the launch traced here: 59.3 us
  Pallas kernels  58 us (98%)
  local copies, waits for them, and re-layouts  1.32 us (2%)
    pallas_call x1, Pallas kernels, shards(): pl.pallas_call(functools.partial(kernel, (n_seq, n_head, stages)), out_sh...  58 us
    unnamed x1, local copies, waits for them, and re-layouts  1.32 us

commit v1 on v0

--- a/solution.py
+++ b/solution.py
@@ -22,24 +22,24 @@
     "Stage", ("last", "far", "near_way", "far_way", "upwards", "split_side", "split_z")
 )
 STAGES = (
-    Stage('x', 4, 0, -1, 1, 0, 0),
-    Stage('y', 0, 0, 0, 4, 0, 1),
-    Stage('y', 4, 0, -1, 6, 0, 1),
-    Stage('x', 0, 0, 1, 4, 0, 0),
+    Stage('x', 4, 0, -1, 7, 1, 1),
+    Stage('y', 0, 0, -1, 4, 1, 1),
+    Stage('y', 4, 0, 1, 6, 1, 1),
+    Stage('x', 0, 0, 1, 5, 1, 0),
 )
 RANKS = (
-    dict(near=11, z=4, far=7, farz=17, over=23, side=2),
-    dict(near=6, z=0, far=9, farz=1, over=13, side=18),
-    dict(near=12, z=21, far=19, farz=3, over=10, side=20),
-    dict(near=16, z=14, far=24, farz=8, over=22, side=5),
+    dict(near=2, z=8, far=10, farz=22, over=9, side=4),
+    dict(near=1, z=7, far=5, farz=0, over=11, side=12),
+    dict(near=6, z=24, far=19, farz=17, over=15, side=23),
+    dict(near=18, z=16, far=3, farz=21, over=20, side=13),
 )
-LATENT_RANK = 15
+LATENT_RANK = 14
 UNITS = 4
 RATE = 46.6e3
-LATENCY = 3.0
+LATENCY = 3.6
 HOP = 0.8
 D2D_RATE = 300e3
-BACKLOG = 1.0
+BACKLOG = 0.5
 SEND_COST = 0.04
 WAIT_COST = 0.02
 BLOCK = 0.8
@@ -486,14 +486,14 @@
         pl.when(j >= middle)(functools.partial(events_of, j, middle, high, back))
 
     def run(b, turn, first, last):
+        if first <= 0 <= last:
+            project_keys(b, turn % 2)
+        if first <= 2 <= last:
+            project_values(b - 2, turn % 2)
         if first <= 1 <= last:
             score(b - 1, (turn - 1) % 2)
         if first <= 2 <= last:
             soften(turn % 2)
-        if first <= 0 <= last:
-            project_keys(b, turn % 2)
-        if first <= 2 <= last:
-            project_values(b - 2, turn % 2)
         if first <= 3 <= last:
             mix(b - 3, (turn - 3) % 2)
             give(b - 3)

time: 59.4 us -> 59.2 us (level)
  no operation moved by 1% of the time
where the time goes in v1:
time: 59.2 us; the launch traced here: 59.1 us
  Pallas kernels  57.8 us (98%)
  local copies, waits for them, and re-layouts  1.32 us (2%)
    pallas_call x1, Pallas kernels, shards(): pl.pallas_call(functools.partial(kernel, (n_seq, n_head, stages)), out_sh...  57.8 us
    unnamed x1, local copies, waits for them, and re-layouts  1.32 us

profile of v1, /device:TPU:1, one launch (start us, length us, event | category | flops | bytes accessed | tf_op | source)
XLA Modules:
  0.0 59.1 jit_solution(9068614546740569945)
XLA Ops:
  0.0 57.8 %shard_map.64 = bf16[128,8192]{1,0:T(8,128)(2,1)S(1)} custom-call(bf16[128,12288]{1,0:T(8,128)(2,1)} %queries.1, bf16[128,512]{1,0:T(8,128)(2,1)} %latent.1, bf16[64,128]{1,0:T(8,128)(2,1)} %bitcast.2, bf16[16,1024]{1,0:T(8,128)(2,1)} %key_weight.1, bf16[16,1024]{1,0:T(8,128)(2,1)} %value_weight.1, s32[1,128]{1,0:T(1,128)} %bitcast.3), custom_call_target="tpu_custom_call" | custom-call | tf_op jit(solution)/shard_map/pallas_call | solution.py:539
  57.8 1.3 %copy.8 = bf16[128,8192]{1,0:T(8,128)(2,1)} copy(bf16[128,8192]{1,0:T(8,128)(2,1)S(1)} %shard_map.64) | data formatting | bytes 4194304

commit v2 on v1

--- a/solution.py
+++ b/solution.py
@@ -498,9 +498,9 @@
             mix(b - 3, (turn - 3) % 2)
             give(b - 3)
 
-    events("setup")
     for xi in range(nx):
         q_copy(xi).start()
+    events("setup")
     setup()
     events("ready")
     for b in range(DEPTH):

time: 59.2 us -> 58.3 us (0.985)
  Pallas kernels: 57.8 us -> 56.8 us
    pallas_call x1, Pallas kernels: 57.8 us -> 56.8 us  [shards(): pl.pallas_call(functools.partial(kernel, (n_seq, n_head, stages)), out_sh...]
where the time goes in v2:
time: 58.3 us; the launch traced here: 58.2 us
  Pallas kernels  56.8 us (97%)
  local copies, waits for them, and re-layouts  1.32 us (2%)
    pallas_call x1, Pallas kernels, shards(): pl.pallas_call(functools.partial(kernel, (n_seq, n_head, stages)), out_sh...  56.8 us
    unnamed x1, local copies, waits for them, and re-layouts  1.32 us

profile of v2, /device:TPU:1, one launch (start us, length us, event | category | flops | bytes accessed | tf_op | source)
XLA Modules:
  0.0 58.2 jit_solution(3095606579173440053)
XLA Ops:
  0.0 56.8 %shard_map.64 = bf16[128,8192]{1,0:T(8,128)(2,1)S(1)} custom-call(bf16[128,12288]{1,0:T(8,128)(2,1)} %queries.1, bf16[128,512]{1,0:T(8,128)(2,1)} %latent.1, bf16[64,128]{1,0:T(8,128)(2,1)} %bitcast.2, bf16[16,1024]{1,0:T(8,128)(2,1)} %key_weight.1, bf16[16,1024]{1,0:T(8,128)(2,1)} %value_weight.1, s32[1,128]{1,0:T(1,128)} %bitcast.3), custom_call_target="tpu_custom_call" | custom-call | tf_op jit(solution)/shard_map/pallas_call | solution.py:539
  56.9 1.3 %copy.8 = bf16[128,8192]{1,0:T(8,128)(2,1)} copy(bf16[128,8192]{1,0:T(8,128)(2,1)S(1)} %shard_map.64) | data formatting | bytes 4194304
